TPU v7x, 32 devices: a whole 2x2x4 slice. The times are simulated.
32 devices in a mesh: dp: 4 (over y, x), fsdp: 8 (over z, core).
Axes of the slice: x: 2, y: 2, z: 4, core: 2. Of those that a mesh axis runs over, the one named last changes fastest.
Arguments:
- latent: bfloat16 [32, 1024, 320], P(('dp', 'fsdp')), may hold values from -6 to 6
- hint: bfloat16 [32, 1024, 320], P(('dp', 'fsdp')), may hold values from -48 to 48
- timestep: int32 [32], P(('dp', 'fsdp')), may hold values from 0 to 999
- skip_grad: bfloat16 [32, 1024, 320], P(('dp', 'fsdp')), may hold values from -6 to 6
- frozen_one: bfloat16 [2880, 320], P('fsdp'), may hold values from -0.109375 to 0.109375
- frozen_two: bfloat16 [2880, 320], P('fsdp'), may hold values from -0.109375 to 0.109375
- time_weight: bfloat16 [320, 1280], P('fsdp'), may hold values from -0.3125 to 0.3125
- frozen_emb: bfloat16 [1280, 320], P('fsdp'), may hold values from -0.15625 to 0.15625
- train_one: bfloat16 [2880, 320], P('fsdp'), may hold values from -0.109375 to 0.109375
- train_two: bfloat16 [2880, 320], P('fsdp'), may hold values from -0.109375 to 0.109375
- train_emb: bfloat16 [1280, 320], P('fsdp'), may hold values from -0.15625 to 0.15625
- zero_weight: bfloat16 [320, 320], P('fsdp'), may hold values from -0.3125 to 0.3125
Outputs:
- skip: bfloat16 [32, 1024, 320], P(('dp', 'fsdp'))
- grad_one: float32 [2880, 320], P('fsdp')
- grad_two: float32 [2880, 320], P('fsdp')
- grad_emb: float32 [1280, 320], P('fsdp')
- grad_zero: float32 [320, 320], P('fsdp')
- grad_norm: float32 [], replicated
All inputs are finite; a program needn't handle non-finite values.
Results may differ from a plain program's by a relative error of at most 0.018.
Values may be sent and summed in bfloat16 or wider, within the bound.
No kernel may reach another device: no remote copies, remote signals or barrier semaphores. Data moves between devices by JAX's collectives and lax.ppermute only.
A program may use at most 128 MiB of HBM per device.

v0:
```python
import math
import jax
import jax.numpy as jnp
from jax import lax
from jax.sharding import PartitionSpec as P

COLS = 64
group_count = 32
clip_limit = 1.0


def conv_apply(flat, kernel):
    count, chans = flat.shape
    height = count // COLS
    padded = jnp.pad(flat.reshape(height, COLS, chans), ((1, 1), (1, 1), (0, 0)))
    total = jnp.zeros((count, kernel.shape[1]), jnp.float32)
    for offset in range(9):
        row_off = offset // 3
        col_off = offset % 3
        piece = padded[row_off : row_off + height, col_off : col_off + COLS].reshape(count, chans)
        total = total + jnp.dot(
            piece, kernel[offset * chans : (offset + 1) * chans], preferred_element_type=jnp.float32
        )
    return total


def conv_back(flat, kernel):
    count, chans = flat.shape
    height = count // COLS
    inner = kernel.shape[0] // 9
    padded = jnp.pad(flat.reshape(height, COLS, chans), ((1, 1), (1, 1), (0, 0)))
    total = jnp.zeros((count, inner), jnp.float32)
    for offset in range(9):
        row_off = offset // 3
        col_off = offset % 3
        piece = padded[
            2 - row_off : 2 - row_off + height, 2 - col_off : 2 - col_off + COLS
        ].reshape(count, chans)
        block = kernel[offset * inner : (offset + 1) * inner]
        total = total + lax.dot_general(
            piece, block, (((1,), (1,)), ((), ())), preferred_element_type=jnp.float32
        )
    return total


def conv_grads(flat, upstream):
    count, chans = flat.shape
    height = count // COLS
    padded = jnp.pad(flat.reshape(height, COLS, chans), ((1, 1), (1, 1), (0, 0)))
    blocks = []
    for offset in range(9):
        row_off = offset // 3
        col_off = offset % 3
        piece = padded[row_off : row_off + height, col_off : col_off + COLS].reshape(count, chans)
        blocks.append(
            lax.dot_general(
                piece, upstream, (((0,), (0,)), ((), ())), preferred_element_type=jnp.float32
            )
        )
    return jnp.concatenate(blocks, axis=0)


def group_norm(value):
    count, chans = value.shape
    grouped = value.reshape(count, group_count, chans // group_count)
    center = jnp.mean(grouped, axis=(0, 2), keepdims=True)
    spread = jnp.mean((grouped - center) ** 2, axis=(0, 2), keepdims=True)
    inverse = lax.rsqrt(spread + 1e-05)
    return (((grouped - center) * inverse).reshape(count, chans), inverse)


def norm_back(upstream, normed, inverse):
    count, chans = upstream.shape
    grouped = upstream.reshape(count, group_count, chans // group_count)
    shaped = normed.reshape(count, group_count, chans // group_count)
    first = jnp.mean(grouped, axis=(0, 2), keepdims=True)
    second = jnp.mean(grouped * shaped, axis=(0, 2), keepdims=True)
    return ((grouped - first - shaped * second) * inverse).reshape(count, chans)


def time_embed(timestep, time_weight):
    half = time_weight.shape[0] // 2
    freqs = jnp.exp(-math.log(10000.0) * jnp.arange(half).astype(jnp.float32) / half)
    angles = timestep.astype(jnp.float32)[:, None] * freqs[None, :]
    wave = jnp.concatenate([jnp.cos(angles), jnp.sin(angles)], axis=1).astype(jnp.bfloat16)
    return jax.nn.silu(jnp.dot(wave, time_weight, preferred_element_type=jnp.float32)).astype(
        jnp.bfloat16
    )


def sample_step(latent_one, hint_one, cotangent, emb_one, weights):
    frozen_one, frozen_two, frozen_emb, train_one, train_two, train_emb, zero_weight = weights
    base = latent_one.astype(jnp.float32)
    emb_row = emb_one[None, :]
    fa0 = jax.nn.silu(group_norm(base)[0]).astype(jnp.bfloat16)
    fp1 = conv_apply(fa0, frozen_one) + jnp.dot(
        emb_row, frozen_emb, preferred_element_type=jnp.float32
    )
    fa1 = jax.nn.silu(group_norm(fp1)[0]).astype(jnp.bfloat16)
    frozen_out = base + conv_apply(fa1, frozen_two)
    mixed_in = base + hint_one.astype(jnp.float32)
    a_zero = jax.nn.silu(group_norm(mixed_in)[0]).astype(jnp.bfloat16)
    p_one = conv_apply(a_zero, train_one) + jnp.dot(
        emb_row, train_emb, preferred_element_type=jnp.float32
    )
    y_one, inverse = group_norm(p_one)
    a_one = jax.nn.silu(y_one).astype(jnp.bfloat16)
    control = (mixed_in + conv_apply(a_one, train_two)).astype(jnp.bfloat16)
    skip_one = (
        frozen_out + jnp.dot(control, zero_weight, preferred_element_type=jnp.float32)
    ).astype(jnp.bfloat16)
    grad_z = lax.dot_general(
        control, cotangent, (((0,), (0,)), ((), ())), preferred_element_type=jnp.float32
    )
    d_control = lax.dot_general(
        cotangent, zero_weight, (((1,), (1,)), ((), ())), preferred_element_type=jnp.float32
    ).astype(jnp.bfloat16)
    grad_w2 = conv_grads(a_one, d_control)
    d_aone = conv_back(d_control, train_two)
    sig = jax.nn.sigmoid(y_one)
    d_yone = d_aone * sig * (1.0 + y_one * (1.0 - sig))
    d_pone = norm_back(d_yone, y_one, inverse)
    grad_e = emb_one.astype(jnp.float32)[:, None] * jnp.sum(d_pone, axis=0)[None, :]
    grad_w1 = conv_grads(a_zero, d_pone.astype(jnp.bfloat16))
    return (skip_one, (grad_w1, grad_w2, grad_e, grad_z))


def run_batch(latent, hint, skip_grad, emb, weights):
    train_one, train_emb, zero_weight = (weights[3], weights[5], weights[6])
    start = (
        jnp.zeros(train_one.shape, jnp.float32),
        jnp.zeros(train_one.shape, jnp.float32),
        jnp.zeros(train_emb.shape, jnp.float32),
        jnp.zeros(zero_weight.shape, jnp.float32),
    )

    def advance(carry, items):
        skip_one, grads = sample_step(items[0], items[1], items[2], items[3], weights)
        return (tuple((old + new for old, new in zip(carry, grads))), skip_one)

    grads, skips = lax.scan(advance, start, (latent, hint, skip_grad, emb))
    return (skips, grads)


def take_rows(whole, shards):
    rows = whole.shape[0] // shards
    return lax.dynamic_slice_in_dim(whole, lax.axis_index("fsdp") * rows, rows, 0)


def body(
    latent,
    hint,
    timestep,
    skip_grad,
    frozen_one,
    frozen_two,
    time_weight,
    frozen_emb,
    train_one,
    train_two,
    train_emb,
    zero_weight,
):
    frozen_full = (
        lax.all_gather(frozen_one, "fsdp", axis=0, tiled=True),
        lax.all_gather(frozen_two, "fsdp", axis=0, tiled=True),
        lax.all_gather(time_weight, "fsdp", axis=0, tiled=True),
        lax.all_gather(frozen_emb, "fsdp", axis=0, tiled=True),
    )
    train_full = (
        lax.all_gather(train_one, "fsdp", axis=0, tiled=True),
        lax.all_gather(train_two, "fsdp", axis=0, tiled=True),
        lax.all_gather(train_emb, "fsdp", axis=0, tiled=True),
        lax.all_gather(zero_weight, "fsdp", axis=0, tiled=True),
    )
    emb = time_embed(timestep, frozen_full[2])
    weights = (
        frozen_full[0],
        frozen_full[1],
        frozen_full[3],
        train_full[0],
        train_full[1],
        train_full[2],
        train_full[3],
    )
    skips, grads = run_batch(latent, hint, skip_grad, emb, weights)
    summed = lax.psum((grads[0], grads[1], grads[2], grads[3]), ("dp", "fsdp"))
    shards = lax.axis_size("fsdp")
    owned = tuple((take_rows(item, shards) for item in summed))
    local_sum = sum((jnp.sum(item * item) for item in owned))
    total = lax.psum(local_sum, "fsdp")
    grad_norm = jnp.sqrt(total + 1e-06)
    scale = jnp.minimum(1.0, clip_limit / grad_norm)
    return (
        skips,
        owned[0] * scale,
        owned[1] * scale,
        owned[2] * scale,
        owned[3] * scale,
        grad_norm,
    )


def solution(mesh):
    in_specs = (
        P(("dp", "fsdp"), None, None),
        P(("dp", "fsdp"), None, None),
        P(("dp", "fsdp")),
        P(("dp", "fsdp"), None, None),
        P("fsdp", None),
        P("fsdp", None),
        P("fsdp", None),
        P("fsdp", None),
        P("fsdp", None),
        P("fsdp", None),
        P("fsdp", None),
        P("fsdp", None),
    )
    out_specs = (
        P(("dp", "fsdp"), None, None),
        P("fsdp", None),
        P("fsdp", None),
        P("fsdp", None),
        P("fsdp", None),
        P(),
    )
    return jax.shard_map(body, mesh=mesh, in_specs=in_specs, out_specs=out_specs, check_vma=False)
```

profile of v0, /device:TPU:0, one launch (start us, length us, event | category | flops | bytes accessed | tf_op | source)
XLA Modules:
  0.0 468.8 jit_solution(11508228289172715350)
XLA Ops:
  14.0 22.5 %all_gather.25 = bf16[320,1280]{1,0:T(8,128)(2,1)S(1)} all-gather(bf16[40,1280]{1,0:T(8,128)(2,1)S(1)} %copy-done.51), channel_id=1, replica_groups=mesh['dp'=4,'fsdp'=8] {'fsdp'}, dimensions={0}, use_global_device_ids=true | all-gather | bytes 921600 | tf_op jit(solution)/shard_map/all_gather | solution.py:167
  36.7 18.6 %all_gather.26 = bf16[1280,320]{1,0:T(8,128)(2,1)S(1)} all-gather(bf16[160,320]{1,0:T(8,128)(2,1)S(1)} %copy-done.49), channel_id=1, replica_groups=mesh['dp'=4,'fsdp'=8] {'fsdp'}, dimensions={0}, use_global_device_ids=true | all-gather | bytes 921600 | tf_op jit(solution)/shard_map/all_gather | solution.py:168
  57.9 22.0 %all_gather.29 = bf16[1280,320]{1,0:T(8,128)(2,1)S(1)} all-gather(bf16[160,320]{1,0:T(8,128)(2,1)S(1)} %copy-done.50), channel_id=1, replica_groups=mesh['dp'=4,'fsdp'=8] {'fsdp'}, dimensions={0}, use_global_device_ids=true | all-gather | bytes 921600 | tf_op jit(solution)/shard_map/all_gather | solution.py:173
  81.8 14.2 %all_gather.31 = bf16[320,320]{1,0:T(8,128)(2,1)S(1)} all-gather(bf16[40,320]{1,0:T(8,128)(2,1)S(1)} %copy-done.52), channel_id=1, replica_groups=mesh['dp'=4,'fsdp'=8] {'fsdp'}, dimensions={0}, use_global_device_ids=true | all-gather | bytes 230400 | tf_op jit(solution)/shard_map/all_gather | solution.py:174
  97.6 3.7 pad_slice_fusion
  101.3 2.9 multiply_convert_fusion
  104.2 6.1 %pad_slice_fusion.16 = (bf16[16,64,320]{2,1,0:T(8,128)(2,1)}, bf16[16,64,320]{2,1,0:T(8,128)(2,1)}, bf16[16,64,320]{2,1,0:T(8,128)(2,1)}, bf16[16,64,320]{2,1,0:...) fusion(bf16[16,64,320]{2,1,0:T(8,128)(2,1)S(1)} %get-tuple-elem, ...), kind=kLoop, calls=%fused_computation.98 | loop fusion | bytes 11796480 | tf_op jit(solution)/shard_map/while/body/eval_jaxpr/slice | solution.py:20
  110.3 4.4 copy.32
  114.7 4.4 reshape.466
  119.1 1.9 fusion.39
  132.6 4.1 copy.34
  136.7 4.6 reshape.468
  141.4 1.9 fusion.96
  151.1 2.1 fusion.101
  154.0 2.6 fusion.103
  169.6 6.2 %pad_slice_fusion.8 = (bf16[16,64,320]{2,1,0:T(8,128)(2,1)S(1)}, bf16[16,64,320]{2,1,0:T(8,128)(2,1)S(1)}, bf16[16,64,320]{2,1,0:T(8,128)(2,1)S(1)}, bf16[16,64,...) fusion(bf16[16,64,320]{2,1,0:T(8,128)(2,1)} %bitcast.244), kind=kLoop, calls=%fused_computation.90 | loop fusion | bytes 5898240 | tf_op jit(solution)/shard_map/while/body/eval_jaxpr/slice | solution.py:54
  193.2 4.1 copy.28
  197.3 4.5 reshape.462
  201.7 4.9 %concatenate.16 = f32[2880,320]{0,1:T(8,128)} concatenate(f32[320,320]{0,1:T(8,128)} %fusion.108, f32[320,320]{0,1:T(8,128)} %fusion.109, f32[320,320]{0,1:T(8,128)} %fusion.110, f32[320,320]{0,1:T(8,128)} %fusion.111, f32[320,320]{0,1:T(8,128)S(1)} %copy-done.46, f32[320,320]{0,1:T(8,128)} %fusion.112, f32[320,320]{0,1:T(8,128)} %fusion.113, f32[320,320]{0,1:T(8,128)} %fusion.114, ...), dimensions={0} | concatenate | bytes 7372800 | tf_op jit(solution)/shard_map/while/body/eval_jaxpr/concatenate | solution.py:60
  206.7 5.1 %concatenate.17 = f32[2880,320]{0,1:T(8,128)} concatenate(f32[320,320]{0,1:T(8,128)} %fusion.116, f32[320,320]{0,1:T(8,128)} %fusion.117, f32[320,320]{0,1:T(8,128)} %fusion.118, f32[320,320]{0,1:T(8,128)} %fusion.119, f32[320,320]{0,1:T(8,128)S(1)} %copy-done.47, f32[320,320]{0,1:T(8,128)} %fusion.120, f32[320,320]{0,1:T(8,128)} %fusion.121, f32[320,320]{0,1:T(8,128)} %fusion.122, ...), dimensions={0} | concatenate | bytes 7372800 | tf_op jit(solution)/shard_map/while/body/eval_jaxpr/concatenate | solution.py:60
  211.8 2.1 fusion.19
  225.7 3.0 fusion.11
  233.2 4.1 copy.30
  237.3 3.4 reshape.464
  240.7 5.9 %pad_slice_fusion.24 = (bf16[16,64,320]{2,1,0:T(8,128)(2,1)S(1)}, bf16[16,64,320]{2,1,0:T(8,128)(2,1)S(1)}, bf16[16,64,320]{2,1,0:T(8,128)(2,1)S(1)}, bf16[16,64...) fusion(bf16[16,64,320]{2,1,0:T(8,128)(2,1)} %bitcast.238), kind=kLoop, calls=%fused_computation.106 | loop fusion | bytes 5898240 | tf_op jit(solution)/shard_map/while/body/eval_jaxpr/slice | solution.py:20
  253.2 171.9 %all-reduce.8.cloned.1.call-done = (f32[2880,320]{0,1:T(8,128)}, f32[2880,320]{0,1:T(8,128)}, f32[1280,320]{1,0:T(8,128)}, f32[320,320]{1,0:T(8,128)}) async-done(((f32[2880,320]{0,1:T(8,128)}, f32[2880,320]{0,1:T(8,128)}, f32[1280,320]{1,0:T(8,128)}, f32[320,320]{1,0:T(8,128)}), (f32[2880,320]{0,1:T(8,128)}, f32[2880,320]{0,1:T(8,128)}, f32[1280,320]{1,0:T(8,128)}, ...) | async-done | bytes 9420816 | tf_op jit(solution)/shard_map/psum | solution.py:187
  425.1 1.9 multiply_reduce_fusion.5
  427.0 1.9 multiply_reduce_fusion.4
  434.6 2.7 fusion.29
  437.3 15.6 %psum.39 = f32[]{:T(128)} all-reduce(f32[]{:T(128)S(6)} %add.398), channel_id=1, replica_groups=mesh['dp'=4,'fsdp'=8] {'fsdp'}, use_global_device_ids=true, to_apply=%region_29.30 | all-reduce | flops 1 | bytes 8 | tf_op jit(solution)/shard_map/psum | solution.py:191
  453.6 2.1 dynamic-slice_multiply_fusion.1
  455.7 2.1 dynamic-slice_multiply_fusion
  (255 shorter events, 91.5 us)
Async XLA Ops:
  7.2 89.5 %copy-start = (bf16[1,1024,320]{1,2,0:T(8,128)(2,1)S(1)}, bf16[1,1024,320]{1,2,0:T(8,128)(2,1)}, u32[]{:S(2)}) copy-start(bf16[1,1024,320]{1,2,0:T(8,128)(2,1)} %param.15) | copy-start | bytes 1966084
  7.2 2.9 copy-start.1
  7.2 103.1 %all-gather.13.cloned.1.call-start = ((), (), s32[]{:S(2)}) async-start(), calls=%async_computation.2 | async-start | bytes 2211840 | tf_op jit(solution)/shard_map/all_gather | solution.py:171
  7.9 124.7 %all-gather.15.cloned.1.call-start = ((), (), s32[]{:S(2)}) async-start(), calls=%async_computation.3 | async-start | bytes 2211840 | tf_op jit(solution)/shard_map/all_gather | solution.py:172
  8.7 184.5 %all-gather.9.cloned.1.call-start = ((), (), s32[]{:S(2)}) async-start(), calls=%async_computation | async-start | bytes 2211840 | tf_op jit(solution)/shard_map/all_gather | solution.py:165
  8.7 2.8 copy-start.4
  9.4 223.8 %all-gather.11.cloned.1.call-start = ((), (), s32[]{:S(2)}) async-start(), calls=%async_computation.1 | async-start | bytes 2211840 | tf_op jit(solution)/shard_map/all_gather | solution.py:166
  10.0 415.1 %all-reduce.8.cloned.1.call-start = ((), (), s32[]{:S(2)}) async-start(), calls=%async_computation.4 | async-start | bytes 19988480 | tf_op jit(solution)/shard_map/psum | solution.py:187
  11.5 2.5 copy-start.51
  12.9 23.8 %copy-start.49 = (bf16[160,320]{1,0:T(8,128)(2,1)S(1)}, bf16[160,320]{1,0:T(8,128)(2,1)}, u32[]{:S(2)}) copy-start(bf16[160,320]{1,0:T(8,128)(2,1)} %param.19) | copy-start | bytes 307204
  55.3 2.5 copy-start.50
  80.1 1.7 copy-start.52
  110.3 15.9 %copy-start.8 = (bf16[16,64,320]{2,1,0:T(8,128)(2,1)}, bf16[16,64,320]{2,1,0:T(8,128)(2,1)S(1)}, u32[]{:S(2)}) copy-start(bf16[16,64,320]{2,1,0:T(8,128)(2,1)S(1)} %get-tuple-element.91) | copy-start | bytes 1966084
  119.1 1.9 copy-start.6
  121.0 1.8 copy-start.18
  136.7 6.5 %copy-start.38 = (bf16[16,64,320]{2,1,0:T(8,128)(2,1)S(1)}, bf16[16,64,320]{2,1,0:T(8,128)(2,1)}, u32[]{:S(2)}) copy-start(bf16[16,64,320]{2,1,0:T(8,128)(2,1)} %get-tuple-element.73) | copy-start | bytes 1966084
  141.3 1.9 copy-start.2
  149.6 1.5 copy-start.48
  154.0 2.6 copy-start.21
  169.6 6.2 %copy-start.3 = (bf16[2880,320]{0,1:T(8,128)(2,1)S(1)}, bf16[2880,320]{0,1:T(8,128)(2,1)}, u32[]{:S(2)}) copy-start(bf16[2880,320]{0,1:T(8,128)(2,1)} %reshape.468) | copy-start | bytes 5529604
  175.8 13.0 %copy-start.22 = (bf16[16,64,320]{2,1,0:T(8,128)(2,1)}, bf16[16,64,320]{2,1,0:T(8,128)(2,1)S(1)}, u32[]{:S(2)}) copy-start(bf16[16,64,320]{2,1,0:T(8,128)(2,1)S(1)} %get-tuple-element.80) | copy-start | bytes 1966084
  197.3 4.5 copy-start.46
  201.7 4.9 %copy-start.47 = (f32[320,320]{0,1:T(8,128)S(1)}, f32[320,320]{0,1:T(8,128)}, u32[]{:S(2)}) copy-start(f32[320,320]{0,1:T(8,128)} %fusion.107) | copy-start | bytes 1228804
  206.7 5.1 %copy-start.23 = (bf16[16,64,320]{2,1,0:T(8,128)(2,1)S(1)}, bf16[16,64,320]{2,1,0:T(8,128)(2,1)}, u32[]{:S(2)}) copy-start(bf16[16,64,320]{2,1,0:T(8,128)(2,1)} %copy-done.22) | copy-start | bytes 1966084
  211.8 3.5 copy-start.7
  213.9 3.0 copy-start.28
  215.3 1.7 copy-start.42
  216.9 1.6 copy-start.41
  218.5 1.7 copy-start.40
  225.7 3.1 copy-start.39
  253.2 181.3 %copy-start.29 = (bf16[1024,320]{0,1:T(8,128)(2,1)S(1)}, bf16[1024,320]{0,1:T(8,128)(2,1)}, u32[]{:S(2)}) copy-start(bf16[1024,320]{0,1:T(8,128)(2,1)} %copy-done.28) | copy-start | bytes 1966084
  253.2 181.3 %copy-start.45 = (bf16[320,320]{1,0:T(8,128)(2,1)S(1)}, bf16[320,320]{1,0:T(8,128)(2,1)}, u32[]{:S(2)}) copy-start(bf16[320,320]{1,0:T(8,128)(2,1)} %copy-done.44) | copy-start | bytes 614404
  (26 other events, 30.9 us)
Sparse Core Ops, SparseCore 0:
  9.6 37.1 all-gather.12
  48.5 36.0 all-gather.14
  86.2 27.3 all-gather.8
  115.2 27.4 all-gather.10
  225.9 199.1 all-reduce.7
where the time goes:
time: 476 us; the launch traced here: 469 us
  waiting for transfers between devices  175 us (37%)
  blocking collectives  92.9 us (20%)
  local copies, waits for them, and re-layouts  83.1 us (17%)
  matrix products  70.8 us (15%)
  other arithmetic  27.4 us (6%)
  between operations  20 us (4%)
    psum x1, waiting for transfers between devices, body(): summed = lax.psum((grads[0], grads[1], grads[2], grads[3]), ('dp', 'fsdp'))  172 us
    dot_general x36, matrix products, conv_apply(): jnp.dot(piece, kernel[offset * chans:(offset + 1) * chans], preferred_ele...  33.7 us
    unnamed x110, local copies, waits for them, and re-layouts  26 us
    dot_general x18, matrix products, conv_grads(): lax.dot_general(piece, upstream, (((0,), (0,)), ((), ())), preferred_elem...  23.7 us
    all_gather x1, blocking collectives, body(): lax.all_gather(time_weight, 'fsdp', axis=0, tiled=True)  22.5 us
    all_gather x1, blocking collectives, body(): lax.all_gather(train_emb, 'fsdp', axis=0, tiled=True)  22 us
    all_gather x1, blocking collectives, body(): lax.all_gather(frozen_emb, 'fsdp', axis=0, tiled=True)  18.6 us
    psum x1, blocking collectives, body(): total = lax.psum(local_sum, 'fsdp')  15.6 us
  transfers between devices with their start and end apart: 5, of which 1 were waited for; matrix products, arithmetic and copies ran while one was open for 33% of the time, Pallas kernels for 0%

commit v1 on v0

--- a/solution.py
+++ b/solution.py
@@ -184,7 +184,7 @@
         train_full[3],
     )
     skips, grads = run_batch(latent, hint, skip_grad, emb, weights)
-    summed = lax.psum((grads[0], grads[1], grads[2], grads[3]), ("dp", "fsdp"))
+    summed = lax.psum(lax.psum((grads[0], grads[1], grads[2], grads[3]), "fsdp"), "dp")
     shards = lax.axis_size("fsdp")
     owned = tuple((take_rows(item, shards) for item in summed))
     local_sum = sum((jnp.sum(item * item) for item in owned))

time: 476 us -> 701 us (1.47)
  waiting for transfers between devices: 175 us -> 409 us
    psum x1 -> x2, waiting for transfers between devices: 172 us -> 386 us  [the longest x1 205 us: body(): lax.psum((grads[0], grads[1], grads[2], grads[3]), 'fsdp')]
    all_gather x1, waiting for transfers between devices: 0.01 us -> 12.5 us  [body(): lax.all_gather(frozen_one, 'fsdp', axis=0, tiled=True)]
    all_gather x1, waiting for transfers between devices: 0.01 us -> 7.94 us  [body(): lax.all_gather(frozen_two, 'fsdp', axis=0, tiled=True)]
    unnamed x110 -> x114, local copies, waits for them, and re-layouts: 26 us -> 28 us
  transfers between devices with their start and end apart: 5 -> 6, of which waited for: 1 -> 4; matrix products, arithmetic and copies ran while one was open for 33% -> 11% of each run, Pallas kernels for 0% -> 0%
where the time goes in v1:
time: 701 us; the launch traced here: 694 us
  waiting for transfers between devices  409 us (58%)
  blocking collectives  89.9 us (13%)
  local copies, waits for them, and re-layouts  84.7 us (12%)
  matrix products  64.4 us (9%)
  other arithmetic  25.4 us (4%)
  between operations  20.4 us (3%)
    psum x1, waiting for transfers between devices, body(): lax.psum((grads[0], grads[1], grads[2], grads[3]), 'fsdp')  205 us
    psum x1, waiting for transfers between devices, body(): lax.psum(lax.psum((grads[0], grads[1], grads[2], grads[3]), 'fsdp'), 'dp')  181 us
    unnamed x114, local copies, waits for them, and re-layouts  28 us
    dot_general x36, matrix products, conv_apply(): jnp.dot(piece, kernel[offset * chans:(offset + 1) * chans], preferred_ele...  27.4 us
    dot_general x18, matrix products, conv_grads(): lax.dot_general(piece, upstream, (((0,), (0,)), ((), ())), preferred_elem...  23.6 us
    all_gather x1, blocking collectives, body(): lax.all_gather(time_weight, 'fsdp', axis=0, tiled=True)  22.5 us
    all_gather x1, blocking collectives, body(): lax.all_gather(frozen_emb, 'fsdp', axis=0, tiled=True)  17.8 us
    all_gather x1, blocking collectives, body(): lax.all_gather(train_emb, 'fsdp', axis=0, tiled=True)  17.5 us
  transfers between devices with their start and end apart: 6, of which 4 were waited for; matrix products, arithmetic and copies ran while one was open for 11% of the time, Pallas kernels for 0%

profile of v1, /device:TPU:0, one launch (start us, length us, event | category | flops | bytes accessed | tf_op | source)
XLA Modules:
  0.0 694.3 jit_solution(11702591857733900415)
XLA Ops:
  8.7 2.5 copy.27
  13.8 22.5 %all_gather.25 = bf16[320,1280]{1,0:T(8,128)(2,1)S(1)} all-gather(bf16[40,1280]{1,0:T(8,128)(2,1)S(1)} %copy-done.53), channel_id=1, replica_groups=mesh['dp'=4,'fsdp'=8] {'fsdp'}, dimensions={0}, use_global_device_ids=true | all-gather | bytes 921600 | tf_op jit(solution)/shard_map/all_gather | solution.py:167
  39.1 17.5 %all_gather.29 = bf16[1280,320]{1,0:T(8,128)(2,1)} all-gather(bf16[160,320]{1,0:T(8,128)(2,1)S(1)} %copy-done.51), channel_id=1, replica_groups=mesh['dp'=4,'fsdp'=8] {'fsdp'}, dimensions={0}, use_global_device_ids=true | all-gather | bytes 921600 | tf_op jit(solution)/shard_map/all_gather | solution.py:173
  58.1 15.4 %all_gather.31 = bf16[320,320]{1,0:T(8,128)(2,1)S(1)} all-gather(bf16[40,320]{1,0:T(8,128)(2,1)S(1)} %copy-done.54), channel_id=1, replica_groups=mesh['dp'=4,'fsdp'=8] {'fsdp'}, dimensions={0}, use_global_device_ids=true | all-gather | bytes 230400 | tf_op jit(solution)/shard_map/all_gather | solution.py:174
  75.0 3.7 pad_slice_fusion
  79.7 6.0 pad_slice_fusion.16
  86.0 4.0 copy.32
  90.0 4.4 reshape.466
  107.9 4.0 copy.34
  111.9 4.6 reshape.468
  126.2 2.1 fusion.101
  129.1 2.6 fusion.103
  144.6 6.1 pad_slice_fusion.8
  171.5 4.8 concatenate.16
  176.3 4.9 concatenate.17
  182.4 204.8 %all-reduce.10.cloned.1.call-done = (f32[2880,320]{0,1:T(8,128)}, f32[2880,320]{0,1:T(8,128)}, f32[1280,320]{1,0:T(8,128)}, f32[320,320]{1,0:T(8,128)}) async-done(((f32[2880,320]{0,1:T(8,128)}, f32[2880,320]{0,1:T(8,128)}, f32[1280,320]{1,0:T(8,128)}, f32[320,320]{1,0:T(8,128)}), (f32[2880,320]{0,1:T(8,128)}, f32[2880,320]{0,1:T(8,128)}, f32[1280,320]{1,0:T(8,128)}, ...) | async-done | bytes 9420816 | tf_op jit(solution)/shard_map/psum | solution.py:187
  388.2 17.8 %all_gather.26 = bf16[1280,320]{1,0:T(8,128)(2,1)S(1)} all-gather(bf16[160,320]{1,0:T(8,128)(2,1)S(1)} %copy-done.52), channel_id=1, replica_groups=mesh['dp'=4,'fsdp'=8] {'fsdp'}, dimensions={0}, use_global_device_ids=true | all-gather | bytes 921600 | tf_op jit(solution)/shard_map/all_gather | solution.py:168
  406.3 12.5 %all-gather.9.cloned.1.call-done = bf16[8,360,320]{1,2,0:T(8,128)(2,1)} async-done(((bf16[1,360,320]{1,2,0:T(8,128)(2,1)}), bf16[8,360,320]{1,2,0:T(8,128)(2,1)}) %all-gather.9.cloned.1.call-update) | async-done | bytes 1843216 | tf_op jit(solution)/shard_map/all_gather | solution.py:165
  418.8 4.0 copy.28
  422.7 3.5 reshape.462
  426.3 2.3 fusion.65
  439.9 7.9 %all-gather.11.cloned.1.call-done = bf16[8,360,320]{1,2,0:T(8,128)(2,1)} async-done(((bf16[1,360,320]{1,2,0:T(8,128)(2,1)}), bf16[8,360,320]{1,2,0:T(8,128)(2,1)}) %all-gather.11.cloned.1.call-update) | async-done | bytes 1843216 | tf_op jit(solution)/shard_map/all_gather | solution.py:166
  447.9 4.0 copy.30
  451.9 3.4 reshape.464
  455.2 5.9 pad_slice_fusion.24
  467.8 181.4 %all-reduce.12.cloned.1.call-done = (f32[2880,320]{0,1:T(8,128)}, f32[2880,320]{0,1:T(8,128)}, f32[1280,320]{1,0:T(8,128)}, f32[320,320]{1,0:T(8,128)}) async-done(((f32[2880,320]{0,1:T(8,128)}, f32[2880,320]{0,1:T(8,128)}, f32[1280,320]{1,0:T(8,128)}, f32[320,320]{1,0:T(8,128)}), (f32[2880,320]{0,1:T(8,128)}, f32[2880,320]{0,1:T(8,128)}, f32[1280,320]{1,0:T(8,128)}, ...) | async-done | bytes 9420816 | tf_op jit(solution)/shard_map/psum | solution.py:187
  649.2 1.9 multiply_reduce_fusion.5
  651.1 1.9 multiply_reduce_fusion.4
  658.7 2.7 fusion.29
  661.4 16.7 %psum.71 = f32[]{:T(128)} all-reduce(f32[]{:T(128)S(6)} %add.406), channel_id=1, replica_groups=mesh['dp'=4,'fsdp'=8] {'fsdp'}, use_global_device_ids=true, to_apply=%region_33.34 | all-reduce | flops 1 | bytes 8 | tf_op jit(solution)/shard_map/psum | solution.py:191
  678.8 2.1 dynamic-slice_multiply_fusion.1
  680.9 2.1 dynamic-slice_multiply_fusion
  (262 shorter events, 94.0 us)
Async XLA Ops:
  7.2 67.0 %copy-start = (bf16[1,1024,320]{1,2,0:T(8,128)(2,1)S(1)}, bf16[1,1024,320]{1,2,0:T(8,128)(2,1)}, u32[]{:S(2)}) copy-start(bf16[1,1024,320]{1,2,0:T(8,128)(2,1)} %param.15) | copy-start | bytes 1966084
  7.2 78.9 %all-gather.13.cloned.1.call-start = ((), (), s32[]{:S(2)}) async-start(), calls=%async_computation.2 | async-start | bytes 2211840 | tf_op jit(solution)/shard_map/all_gather | solution.py:171
  7.2 4.0 copy-start.4
  7.9 100.0 %all-gather.15.cloned.1.call-start = ((), (), s32[]{:S(2)}) async-start(), calls=%async_computation.3 | async-start | bytes 2211840 | tf_op jit(solution)/shard_map/all_gather | solution.py:172
  8.7 378.6 %all-reduce.10.cloned.1.call-start = ((), (), s32[]{:S(2)}) async-start(), calls=%async_computation.4 | async-start | bytes 19988480 | tf_op jit(solution)/shard_map/psum | solution.py:187
  11.2 1.5 copy-start.1
  11.2 2.5 copy-start.53
  36.5 2.6 copy-start.51
  39.1 18.9 %copy-start.54 = (bf16[40,320]{1,0:T(8,128)(2,1)S(1)}, bf16[40,320]{1,0:T(8,128)(2,1)}, u32[]{:S(2)}) copy-start(bf16[40,320]{1,0:T(8,128)(2,1)} %param.23) | copy-start | bytes 76804
  75.0 3.7 copy-start.22
  75.0 3.7 copy-start.23
  79.7 6.0 copy-start.30
  85.7 15.8 %copy-start.8 = (bf16[16,64,320]{2,1,0:T(8,128)(2,1)}, bf16[16,64,320]{2,1,0:T(8,128)(2,1)S(1)}, u32[]{:S(2)}) copy-start(bf16[16,64,320]{2,1,0:T(8,128)(2,1)S(1)} %get-tuple-element.95) | copy-start | bytes 1966084
  94.4 1.9 copy-start.6
  96.3 1.8 copy-start.18
  111.9 6.5 copy-start.39
  116.4 1.9 copy-start.2
  124.6 1.5 copy-start.50
  129.1 2.6 copy-start.21
  144.6 6.1 copy-start.3
  169.7 1.6 copy-start.46
  169.7 1.6 copy-start.48
  169.7 1.8 copy-start.49
  171.5 4.8 copy-start.47
  181.2 237.5 %all-gather.9.cloned.1.call-start = ((), (), s32[]{:S(2)}) async-start(), calls=%async_computation | async-start | bytes 2211840 | tf_op jit(solution)/shard_map/all_gather | solution.py:165
  181.8 266.1 %all-gather.11.cloned.1.call-start = ((), (), s32[]{:S(2)}) async-start(), calls=%async_computation.1 | async-start | bytes 2211840 | tf_op jit(solution)/shard_map/all_gather | solution.py:166
  182.4 466.9 %all-reduce.12.cloned.1.call-start = ((), (), s32[]{:S(2)}) async-start(), calls=%async_computation.5 | async-start | bytes 19988480 | tf_op jit(solution)/shard_map/psum | solution.py:187
  426.3 8.0 %copy-start.7 = (bf16[2880,320]{0,1:T(8,128)(2,1)}, bf16[2880,320]{0,1:T(8,128)(2,1)S(1)}, u32[]{:S(2)}) copy-start(bf16[2880,320]{0,1:T(8,128)(2,1)S(1)} %reshape.462) | copy-start | bytes 5529604
  426.3 2.4 copy-start.43
  438.7 9.1 %copy-start.26 = (bf16[1024,320]{0,1:T(8,128)(2,1)}, bf16[1024,320]{0,1:T(8,128)(2,1)S(1)}, u32[]{:S(2)}) copy-start(bf16[1024,320]{0,1:T(8,128)(2,1)S(1)} %multiply_convert_fusion.4) | copy-start | bytes 1966084
  467.8 190.9 %copy-start.29 = (bf16[1024,320]{0,1:T(8,128)(2,1)S(1)}, bf16[1024,320]{0,1:T(8,128)(2,1)}, u32[]{:S(2)}) copy-start(bf16[1024,320]{0,1:T(8,128)(2,1)} %copy-done.28) | copy-start | bytes 1966084
  467.8 190.9 %copy-start.45 = (bf16[320,320]{1,0:T(8,128)(2,1)S(1)}, bf16[320,320]{1,0:T(8,128)(2,1)}, u32[]{:S(2)}) copy-start(bf16[320,320]{1,0:T(8,128)(2,1)} %copy-done.44) | copy-start | bytes 614404
  (29 other events, 33.8 us)
Sparse Core Ops, SparseCore 0:
  9.6 34.8 all-gather.12
  46.2 30.3 all-gather.14
  181.3 205.8 all-reduce.9
  388.8 29.9 all-gather.8
  420.2 27.5 all-gather.10
  451.7 197.4 all-reduce.11
